TPU v7x, 256 devices: a whole 4x4x8 slice. The times are simulated.
256 devices in a mesh: gy: 8 (over z), gz: 32 (over x, y, core).
Axes of the slice: x: 4, y: 4, z: 8, core: 2. Of those that a mesh axis runs over, the one named last changes fastest.
Arguments:
- data_weight: float32 [640, 640, 640], P('gy', 'gz'), may hold values from 0.25 to 4
- blob_taps: float32 [3, 7], replicated, may hold values from 0.2 to 1
Outputs:
- new_weight: float32 [640, 640, 640], P('gy', 'gz')
- changes: float32 [3], replicated
All inputs are finite; a program needn't handle non-finite values.
Results may differ from a plain program's by a relative error of at most 0.00002.
Values sent between devices are 32-bit elements; how exact they have to be, the bound alone decides.
A program may use at most 64 MiB of HBM per device.

v0:
```python
import jax
import jax.numpy as jnp
from jax import lax
from jax.sharding import Mesh
from jax.sharding import PartitionSpec as P

RAD = 3
ITERS = 3
GZ = ("gz_0", "gz_1", "gz_2")
GY_GZ = ("gy", "gz_0", "gz_1", "gz_2")


def with_halo(cells, sides, width):
    for axis, dim in sides:
        count = lax.axis_size(axis)
        ends = count - 1
        head = lax.slice_in_dim(cells, 0, width, axis=dim)
        tail = lax.slice_in_dim(cells, cells.shape[dim] - width, cells.shape[dim], axis=dim)
        cells = jnp.concatenate(
            [
                lax.ppermute(tail, axis, [(i, (i + 1) % count) for i in range(ends)]),
                cells,
                lax.ppermute(head, axis, [((i + 1) % count, i) for i in range(ends)]),
            ],
            axis=dim,
        )
    return cells


def over_axes(value, axes):
    for axis in axes:
        value = lax.pmax(value, axis)
    return value


def smear_valid(padded, kernel, axis_dim):
    length = padded.shape[axis_dim] - 2 * RAD
    result = kernel[0] * lax.slice_in_dim(padded, 0, length, axis=axis_dim)
    for offset in range(1, 2 * RAD + 1):
        result = result + kernel[offset] * lax.slice_in_dim(
            padded, offset, offset + length, axis=axis_dim
        )
    return result


def smear_local(field, kernel):
    padded = jnp.pad(field, ((0, 0), (0, 0), (RAD, RAD)))
    return smear_valid(padded, kernel, 2)


def shards(data_weight, blob_taps):
    kernel = blob_taps / jnp.sum(blob_taps, axis=1, keepdims=True)
    local_max = []
    weight = jnp.ones_like(data_weight)
    for iteration in range(ITERS):
        product = weight * data_weight
        blurred = smear_local(product, kernel[2])
        padded = with_halo(blurred, (("gy", 0),), RAD)
        blurred = smear_valid(padded, kernel[0], 0)
        padded = with_halo(blurred, ((GZ, 1),), RAD)
        blurred = smear_valid(padded, kernel[1], 1)
        weight = weight / blurred
        deviation = jnp.max(jnp.abs(blurred - 1.0))
        local_max.append(deviation)
    result_max = over_axes(jnp.stack(local_max), GY_GZ)
    return (weight, result_max)


def solution(mesh):
    finer = Mesh(mesh.devices.reshape(mesh.shape["gy"], 4, 4, 2), ("gy", "gz_0", "gz_1", "gz_2"))
    return jax.shard_map(
        shards,
        mesh=finer,
        in_specs=(P("gy", GZ, None), P()),
        out_specs=(P("gy", GZ, None), P()),
        check_vma=False,
    )
```

profile of v0, /device:TPU:1, one launch (start us, length us, event | category | flops | bytes accessed | tf_op | source)
XLA Modules:
  0.0 279.5 jit_solution(7314912291273884327)
XLA Ops:
  3.5 21.4 %fusion.90 = f32[80,20,640]{2,0,1:T(8,128)S(1)} fusion(f32[80,20,640]{2,0,1:T(8,128)} %param.2, f32[]{:T(128)} %bitcast.8, f32[]{:T(128)} %bitcast.7, f32[]{:T(128)} %bitcast.6, f32[]{:T(128)} %bitcast.5, f32[]{:T(128)} %bitcast.4, f32[]{:T(128)} %bitcast.3, f32[]{:T(128)} %bitcast.2), kind=kLoop, calls=%fused_computation.156 | loop fusion | flops 13312000 | bytes 8192028 | tf_op jit(solution)/shard_map/add | solution.py:40
  25.0 4.4 %collective-permute-start = (f32[3,20,640]{2,0,1:T(4,128)S(1)}, f32[3,20,640]{2,0,1:T(4,128)S(1)}, u32[]{:S(2)}, u32[]{:S(2)}) collective-permute-start(f32[3,20,640]{2,0,1:T(4,128)S(1)} %get-tuple-element.20), channel_id=1, source_target_pairs={{0,32},{32,64},{64,96},{96,128},{128,160},{160,192},{192,224},{1,3... | collective-permute-start | bytes 460808 | tf_op jit(solution)/shard_map/ppermute | solution.py:21
  30.7 2.4 collective-permute-done
  33.1 4.2 %collective-permute-done.1 = f32[3,20,640]{2,0,1:T(4,128)S(1)} collective-permute-done((f32[3,20,640]{2,0,1:T(4,128)S(1)}, f32[3,20,640]{2,0,1:T(4,128)S(1)}, u32[]{:S(2)}, u32[]{:S(2)}) %collective-permute-start.1) | collective-permute-done | bytes 153632 | tf_op jit(solution)/shard_map/ppermute | solution.py:23
  37.3 8.1 %fusion.31 = f32[80,20,640]{2,0,1:T(8,128)S(1)} fusion(f32[80,20,640]{2,0,1:T(8,128)S(1)} %fusion.90, f32[3,20,640]{2,0,1:T(4,128)S(1)} %collective-permute-done.1, f32[3,20,640]{2,0,1:T(4,128)S(1)} %collective-permute-done, f32[]{:T(128)} %bitcast.14, f32[]{:T(128)} %bitcast.13, f32[]{:T(128)} %bitcast.12, f32[]{:T(128)} %bitcast.11, f32[]{:T(128)} %bitcast.10, ...), kind=kLoop, calls=%fused_computation.97 | loop fusion | flops 19456000 | bytes 8499228 | tf_op jit(solution)/shard_map/add | solution.py:40
  45.6 4.7 %collective-permute-start.2 = (f32[80,3,640]{2,0,1:T(8,128)S(1)}, f32[80,3,640]{2,0,1:T(8,128)S(1)}, u32[]{:S(2)}, u32[]{:S(2)}) collective-permute-start(f32[80,3,640]{2,0,1:T(8,128)S(1)} %get-tuple-element.18), channel_id=1, source_target_pairs={{0,1},{1,2},{2,3},{3,4},{4,5},{5,6},{6,7},{7,8},{8,9},{9,10},{10,1... | collective-permute-start | bytes 1843208 | tf_op jit(solution)/shard_map/ppermute | solution.py:21
  52.3 5.1 %collective-permute-done.2 = f32[80,3,640]{2,0,1:T(8,128)S(1)} collective-permute-done((f32[80,3,640]{2,0,1:T(8,128)S(1)}, f32[80,3,640]{2,0,1:T(8,128)S(1)}, u32[]{:S(2)}, u32[]{:S(2)}) %collective-permute-start.2) | collective-permute-done | bytes 614432 | tf_op jit(solution)/shard_map/ppermute | solution.py:21
  57.4 4.4 %collective-permute-done.3 = f32[80,3,640]{2,0,1:T(8,128)S(1)} collective-permute-done((f32[80,3,640]{2,0,1:T(8,128)S(1)}, f32[80,3,640]{2,0,1:T(8,128)S(1)}, u32[]{:S(2)}, u32[]{:S(2)}) %collective-permute-start.3) | collective-permute-done | bytes 614432 | tf_op jit(solution)/shard_map/ppermute | solution.py:23
  61.8 16.6 %abs_reduce_fusion.2 = (f32[]{:T(128)}, f32[80,20,640]{2,0,1:T(8,128)S(1)}) fusion(f32[80,3,640]{2,0,1:T(8,128)S(1)} %collective-permute-done.3, f32[80,20,640]{2,0,1:T(8,128)} %copy-done.1, f32[]{:T(128)} %bitcast.20, f32[]{:T(128)} %bitcast.19, f32[]{:T(128)} %bitcast.18, f32[]{:T(128)} %bitcast.17, f32[80,3,640]{2,0,1:T(8,128)S(1)} %collective-permute-done.2, ...), kind=kLoop, calls=%fused_computation.212 | loop fusion | flops 22528000 | bytes 9420832 | tf_op jit(solution)/shard_map/reduce_max | solution.py:63
  78.4 2.5 divide_multiply_fusion.1
  80.9 21.3 %fusion.102 = f32[80,20,640]{2,0,1:T(8,128)S(1)} fusion(f32[80,20,640]{2,0,1:T(8,128)} %divide_multiply_fusion.1, f32[]{:T(128)} %bitcast.8, f32[]{:T(128)} %bitcast.7, f32[]{:T(128)} %bitcast.6, f32[]{:T(128)} %bitcast.5, f32[]{:T(128)} %bitcast.4, f32[]{:T(128)} %bitcast.3, f32[]{:T(128)} %bitcast.2), kind=kLoop, calls=%fused_computation.168 | loop fusion | flops 13312000 | bytes 8192028 | tf_op jit(solution)/shard_map/add | solution.py:40
  102.3 3.6 %collective-permute-start.4 = (f32[3,20,640]{2,0,1:T(4,128)S(1)}, f32[3,20,640]{2,0,1:T(4,128)S(1)}, u32[]{:S(2)}, u32[]{:S(2)}) collective-permute-start(f32[3,20,640]{2,0,1:T(4,128)S(1)} %get-tuple-element.16), channel_id=1, source_target_pairs={{0,32},{32,64},{64,96},{96,128},{128,160},{160,192},{192,224},{1,3... | collective-permute-start | bytes 460808 | tf_op jit(solution)/shard_map/ppermute | solution.py:21
  108.5 5.2 %collective-permute-done.5 = f32[3,20,640]{2,0,1:T(4,128)S(1)} collective-permute-done((f32[3,20,640]{2,0,1:T(4,128)S(1)}, f32[3,20,640]{2,0,1:T(4,128)S(1)}, u32[]{:S(2)}, u32[]{:S(2)}) %collective-permute-start.5) | collective-permute-done | bytes 153632 | tf_op jit(solution)/shard_map/ppermute | solution.py:23
  113.7 8.1 %fusion.17 = f32[80,20,640]{2,0,1:T(8,128)S(1)} fusion(f32[80,20,640]{2,0,1:T(8,128)S(1)} %fusion.102, f32[3,20,640]{2,0,1:T(4,128)S(1)} %collective-permute-done.5, f32[3,20,640]{2,0,1:T(4,128)S(1)} %collective-permute-done.4, f32[]{:T(128)} %bitcast.14, f32[]{:T(128)} %bitcast.13, f32[]{:T(128)} %bitcast.12, f32[]{:T(128)} %bitcast.11, f32[]{:T(128)} %bitcast.10, ...), kind=kLoop, calls=%fused_computation.83 | loop fusion | flops 19456000 | bytes 8499228 | tf_op jit(solution)/shard_map/add | solution.py:40
  124.0 4.4 %collective-permute-start.6 = (f32[80,3,640]{2,0,1:T(8,128)S(1)}, f32[80,3,640]{2,0,1:T(8,128)S(1)}, u32[]{:S(2)}, u32[]{:S(2)}) collective-permute-start(f32[80,3,640]{2,0,1:T(8,128)S(1)} %get-tuple-element.14), channel_id=1, source_target_pairs={{0,1},{1,2},{2,3},{3,4},{4,5},{5,6},{6,7},{7,8},{8,9},{9,10},{10,1... | collective-permute-start | bytes 1843208 | tf_op jit(solution)/shard_map/ppermute | solution.py:21
  130.3 5.1 %collective-permute-done.6 = f32[80,3,640]{2,0,1:T(8,128)S(1)} collective-permute-done((f32[80,3,640]{2,0,1:T(8,128)S(1)}, f32[80,3,640]{2,0,1:T(8,128)S(1)}, u32[]{:S(2)}, u32[]{:S(2)}) %collective-permute-start.6) | collective-permute-done | bytes 614432 | tf_op jit(solution)/shard_map/ppermute | solution.py:21
  135.4 4.4 %collective-permute-done.7 = f32[80,3,640]{2,0,1:T(8,128)S(1)} collective-permute-done((f32[80,3,640]{2,0,1:T(8,128)S(1)}, f32[80,3,640]{2,0,1:T(8,128)S(1)}, u32[]{:S(2)}, u32[]{:S(2)}) %collective-permute-start.7) | collective-permute-done | bytes 614432 | tf_op jit(solution)/shard_map/ppermute | solution.py:23
  139.8 17.6 %abs_reduce_fusion.1 = (f32[]{:T(128)}, f32[80,20,640]{2,0,1:T(8,128)}) fusion(f32[80,3,640]{2,0,1:T(8,128)S(1)} %collective-permute-done.7, f32[80,20,640]{2,0,1:T(8,128)} %copy-done.2, f32[]{:T(128)} %bitcast.20, f32[]{:T(128)} %bitcast.19, f32[]{:T(128)} %bitcast.18, f32[]{:T(128)} %bitcast.17, f32[80,3,640]{2,0,1:T(8,128)S(1)} %collective-permute-done.6, ...), kind=kLoop, calls=%fused_computation.211 | loop fusion | flops 22528000 | bytes 9420832 | tf_op jit(solution)/shard_map/reduce_max | solution.py:63
  157.4 6.3 %divide_multiply_fusion = (f32[80,20,640]{2,0,1:T(8,128)}, f32[80,20,640]{2,0,1:T(8,128)}) fusion(f32[80,20,640]{2,0,1:T(8,128)S(1)} %copy-done, f32[80,20,640]{2,0,1:T(8,128)S(1)} %get-tuple-element.3, f32[80,20,640]{2,0,1:T(8,128)} %get-tuple-element.5), kind=kLoop, calls=%fused_computation.214 | loop fusion | flops 3072000 | bytes 20480000 | tf_op jit(solution)/shard_map/mul | solution.py:56
  163.6 21.3 %fusion.114 = f32[80,20,640]{2,0,1:T(8,128)S(1)} fusion(f32[80,20,640]{2,0,1:T(8,128)} %get-tuple-element.8, f32[]{:T(128)} %bitcast.8, f32[]{:T(128)} %bitcast.7, f32[]{:T(128)} %bitcast.6, f32[]{:T(128)} %bitcast.5, f32[]{:T(128)} %bitcast.4, f32[]{:T(128)} %bitcast.3, f32[]{:T(128)} %bitcast.2), kind=kLoop, calls=%fused_computation.180 | loop fusion | flops 13312000 | bytes 8192028 | tf_op jit(solution)/shard_map/add | solution.py:40
  185.0 4.6 %collective-permute-start.8 = (f32[3,20,640]{2,0,1:T(4,128)S(1)}, f32[3,20,640]{2,0,1:T(4,128)S(1)}, u32[]{:S(2)}, u32[]{:S(2)}) collective-permute-start(f32[3,20,640]{2,0,1:T(4,128)S(1)} %get-tuple-element.12), channel_id=1, source_target_pairs={{0,32},{32,64},{64,96},{96,128},{128,160},{160,192},{192,224},{1,3... | collective-permute-start | bytes 460808 | tf_op jit(solution)/shard_map/ppermute | solution.py:21
  192.3 4.4 %collective-permute-done.9 = f32[3,20,640]{2,0,1:T(4,128)S(1)} collective-permute-done((f32[3,20,640]{2,0,1:T(4,128)S(1)}, f32[3,20,640]{2,0,1:T(4,128)S(1)}, u32[]{:S(2)}, u32[]{:S(2)}) %collective-permute-start.9) | collective-permute-done | bytes 153632 | tf_op jit(solution)/shard_map/ppermute | solution.py:23
  196.6 8.1 %fusion.3 = f32[80,20,640]{2,0,1:T(8,128)S(1)} fusion(f32[80,20,640]{2,0,1:T(8,128)S(1)} %fusion.114, f32[3,20,640]{2,0,1:T(4,128)S(1)} %collective-permute-done.9, f32[3,20,640]{2,0,1:T(4,128)S(1)} %collective-permute-done.8, f32[]{:T(128)} %bitcast.14, f32[]{:T(128)} %bitcast.13, f32[]{:T(128)} %bitcast.12, f32[]{:T(128)} %bitcast.11, f32[]{:T(128)} %bitcast.10, ...), kind=kLoop, calls=%fused_computation.69 | loop fusion | flops 19456000 | bytes 8499228 | tf_op jit(solution)/shard_map/add | solution.py:40
  204.9 3.9 %collective-permute-start.10 = (f32[80,3,640]{2,0,1:T(8,128)S(1)}, f32[80,3,640]{2,0,1:T(8,128)S(1)}, u32[]{:S(2)}, u32[]{:S(2)}) collective-permute-start(f32[80,3,640]{2,0,1:T(8,128)S(1)} %get-tuple-element.10), channel_id=1, source_target_pairs={{0,1},{1,2},{2,3},{3,4},{4,5},{5,6},{6,7},{7,8},{8,9},{9,10},{10,1... | collective-permute-start | bytes 1843208 | tf_op jit(solution)/shard_map/ppermute | solution.py:21
  210.7 5.1 %collective-permute-done.10 = f32[80,3,640]{2,0,1:T(8,128)S(1)} collective-permute-done((f32[80,3,640]{2,0,1:T(8,128)S(1)}, f32[80,3,640]{2,0,1:T(8,128)S(1)}, u32[]{:S(2)}, u32[]{:S(2)}) %collective-permute-start.10) | collective-permute-done | bytes 614432 | tf_op jit(solution)/shard_map/ppermute | solution.py:21
  215.9 4.4 %collective-permute-done.11 = f32[80,3,640]{2,0,1:T(8,128)S(1)} collective-permute-done((f32[80,3,640]{2,0,1:T(8,128)S(1)}, f32[80,3,640]{2,0,1:T(8,128)S(1)}, u32[]{:S(2)}, u32[]{:S(2)}) %collective-permute-start.11) | collective-permute-done | bytes 614432 | tf_op jit(solution)/shard_map/ppermute | solution.py:23
  220.3 11.4 %abs_reduce_fusion = (f32[]{:T(128)}, f32[80,20,640]{2,0,1:T(8,128)}) fusion(f32[80,3,640]{2,0,1:T(8,128)S(1)} %collective-permute-done.11, f32[80,20,640]{2,0,1:T(8,128)S(1)} %fusion.3, f32[]{:T(128)} %bitcast.20, f32[]{:T(128)} %bitcast.19, f32[]{:T(128)} %bitcast.18, f32[]{:T(128)} %bitcast.17, f32[80,3,640]{2,0,1:T(8,128)S(1)} %collective-permute-done.10, ...), kind=kLoop, calls=%fused_computation.210 | loop fusion | flops 22528000 | bytes 9420832 | tf_op jit(solution)/shard_map/reduce_max | solution.py:63
  233.5 12.7 %pmax.28 = f32[3]{0:T(128)S(1)} all-reduce(f32[3]{0:T(128)S(1)} %pad_maximum_fusion.12), channel_id=1, replica_groups=mesh['gy'=8,'gz_0'=4,'gz_1'=4,'gz_2'=2] {'gy'}, use_global_device_ids=true, to_apply=%region_4.5 | all-reduce | flops 3 | bytes 24 | tf_op jit(solution)/shard_map/pmax | solution.py:32
  246.2 8.8 %pmax.29 = f32[3]{0:T(128)S(1)} all-reduce(f32[3]{0:T(128)S(1)} %pmax.28), channel_id=1, replica_groups=mesh['gy'=8,'gz_0'=4,'gz_1'=4,'gz_2'=2] {'gz_0'}, use_global_device_ids=true, to_apply=%region_5.6 | all-reduce | flops 3 | bytes 24 | tf_op jit(solution)/shard_map/pmax | solution.py:32
  255.0 10.8 %pmax.30 = f32[3]{0:T(128)S(1)} all-reduce(f32[3]{0:T(128)S(1)} %pmax.29), channel_id=1, replica_groups=mesh['gy'=8,'gz_0'=4,'gz_1'=4,'gz_2'=2] {'gz_1'}, use_global_device_ids=true, to_apply=%region_6.7 | all-reduce | flops 3 | bytes 24 | tf_op jit(solution)/shard_map/pmax | solution.py:32
  265.8 7.8 %pmax.31 = f32[3]{0:T(128)} all-reduce(f32[3]{0:T(128)S(1)} %pmax.30), channel_id=1, replica_groups=mesh['gy'=8,'gz_0'=4,'gz_1'=4,'gz_2'=2] {'gz_2'}, use_global_device_ids=true, to_apply=%region_7.8 | all-reduce | flops 3 | bytes 24 | tf_op jit(solution)/shard_map/pmax | solution.py:32
  273.6 5.9 %multiply_divide_fusion = f32[80,20,640]{2,0,1:T(8,128)} fusion(f32[80,20,640]{2,0,1:T(8,128)} %get-tuple-element.9, f32[80,20,640]{2,0,1:T(8,128)} %get-tuple-element.7), kind=kLoop, calls=%fused_computation.213 | loop fusion | flops 2048000 | bytes 12288000 | tf_op jit(solution)/shard_map/div | solution.py:62
  (25 shorter events, 19.6 us)
Async XLA Ops:
  25.0 8.1 %collective-permute-start = (f32[3,20,640]{2,0,1:T(4,128)S(1)}, f32[3,20,640]{2,0,1:T(4,128)S(1)}, u32[]{:S(2)}, u32[]{:S(2)}) collective-permute-start(f32[3,20,640]{2,0,1:T(4,128)S(1)} %get-tuple-element.20), channel_id=1, source_target_pairs={{0,32},{32,64},{64,96},{96,128},{128,160},{160,192},{192,224},{1,3... | collective-permute-start | bytes 460808 | tf_op jit(solution)/shard_map/ppermute | solution.py:21
  29.4 7.9 %collective-permute-start.1 = (f32[3,20,640]{2,0,1:T(4,128)S(1)}, f32[3,20,640]{2,0,1:T(4,128)S(1)}, u32[]{:S(2)}, u32[]{:S(2)}) collective-permute-start(f32[3,20,640]{2,0,1:T(4,128)S(1)} %get-tuple-element.21), channel_id=1, source_target_pairs={{32,0},{64,32},{96,64},{128,96},{160,128},{192,160},{224,192},{33,... | collective-permute-start | bytes 460808 | tf_op jit(solution)/shard_map/ppermute | solution.py:23
  45.5 16.3 %copy-start.1 = (f32[80,20,640]{2,0,1:T(8,128)}, f32[80,20,640]{2,0,1:T(8,128)S(1)}, u32[]{:S(2)}) copy-start(f32[80,20,640]{2,0,1:T(8,128)S(1)} %fusion.31) | copy-start | bytes 12288004
  45.6 11.8 %collective-permute-start.2 = (f32[80,3,640]{2,0,1:T(8,128)S(1)}, f32[80,3,640]{2,0,1:T(8,128)S(1)}, u32[]{:S(2)}, u32[]{:S(2)}) collective-permute-start(f32[80,3,640]{2,0,1:T(8,128)S(1)} %get-tuple-element.18), channel_id=1, source_target_pairs={{0,1},{1,2},{2,3},{3,4},{4,5},{5,6},{6,7},{7,8},{8,9},{9,10},{10,1... | collective-permute-start | bytes 1843208 | tf_op jit(solution)/shard_map/ppermute | solution.py:21
  50.3 11.5 %collective-permute-start.3 = (f32[80,3,640]{2,0,1:T(8,128)S(1)}, f32[80,3,640]{2,0,1:T(8,128)S(1)}, u32[]{:S(2)}, u32[]{:S(2)}) collective-permute-start(f32[80,3,640]{2,0,1:T(8,128)S(1)} %get-tuple-element.19), channel_id=1, source_target_pairs={{1,0},{2,1},{3,2},{4,3},{5,4},{6,5},{7,6},{8,7},{9,8},{10,9},{11,1... | collective-permute-start | bytes 1843208 | tf_op jit(solution)/shard_map/ppermute | solution.py:23
  61.8 16.6 %copy-start = (f32[80,20,640]{2,0,1:T(8,128)S(1)}, f32[80,20,640]{2,0,1:T(8,128)}, u32[]{:S(2)}) copy-start(f32[80,20,640]{2,0,1:T(8,128)} %param.2) | copy-start | bytes 12288004
  102.3 6.2 %collective-permute-start.4 = (f32[3,20,640]{2,0,1:T(4,128)S(1)}, f32[3,20,640]{2,0,1:T(4,128)S(1)}, u32[]{:S(2)}, u32[]{:S(2)}) collective-permute-start(f32[3,20,640]{2,0,1:T(4,128)S(1)} %get-tuple-element.16), channel_id=1, source_target_pairs={{0,32},{32,64},{64,96},{96,128},{128,160},{160,192},{192,224},{1,3... | collective-permute-start | bytes 460808 | tf_op jit(solution)/shard_map/ppermute | solution.py:21
  105.9 7.9 %collective-permute-start.5 = (f32[3,20,640]{2,0,1:T(4,128)S(1)}, f32[3,20,640]{2,0,1:T(4,128)S(1)}, u32[]{:S(2)}, u32[]{:S(2)}) collective-permute-start(f32[3,20,640]{2,0,1:T(4,128)S(1)} %get-tuple-element.17), channel_id=1, source_target_pairs={{32,0},{64,32},{96,64},{128,96},{160,128},{192,160},{224,192},{33,... | collective-permute-start | bytes 460808 | tf_op jit(solution)/shard_map/ppermute | solution.py:23
  121.9 2.0 copy-start.2
  124.0 11.5 %collective-permute-start.6 = (f32[80,3,640]{2,0,1:T(8,128)S(1)}, f32[80,3,640]{2,0,1:T(8,128)S(1)}, u32[]{:S(2)}, u32[]{:S(2)}) collective-permute-start(f32[80,3,640]{2,0,1:T(8,128)S(1)} %get-tuple-element.14), channel_id=1, source_target_pairs={{0,1},{1,2},{2,3},{3,4},{4,5},{5,6},{6,7},{7,8},{8,9},{9,10},{10,1... | collective-permute-start | bytes 1843208 | tf_op jit(solution)/shard_map/ppermute | solution.py:21
  128.4 11.5 %collective-permute-start.7 = (f32[80,3,640]{2,0,1:T(8,128)S(1)}, f32[80,3,640]{2,0,1:T(8,128)S(1)}, u32[]{:S(2)}, u32[]{:S(2)}) collective-permute-start(f32[80,3,640]{2,0,1:T(8,128)S(1)} %get-tuple-element.15), channel_id=1, source_target_pairs={{1,0},{2,1},{3,2},{4,3},{5,4},{6,5},{7,6},{8,7},{9,8},{10,9},{11,1... | collective-permute-start | bytes 1843208 | tf_op jit(solution)/shard_map/ppermute | solution.py:23
  185.0 7.3 %collective-permute-start.8 = (f32[3,20,640]{2,0,1:T(4,128)S(1)}, f32[3,20,640]{2,0,1:T(4,128)S(1)}, u32[]{:S(2)}, u32[]{:S(2)}) collective-permute-start(f32[3,20,640]{2,0,1:T(4,128)S(1)} %get-tuple-element.12), channel_id=1, source_target_pairs={{0,32},{32,64},{64,96},{96,128},{128,160},{160,192},{192,224},{1,3... | collective-permute-start | bytes 460808 | tf_op jit(solution)/shard_map/ppermute | solution.py:21
  189.6 7.1 %collective-permute-start.9 = (f32[3,20,640]{2,0,1:T(4,128)S(1)}, f32[3,20,640]{2,0,1:T(4,128)S(1)}, u32[]{:S(2)}, u32[]{:S(2)}) collective-permute-start(f32[3,20,640]{2,0,1:T(4,128)S(1)} %get-tuple-element.13), channel_id=1, source_target_pairs={{32,0},{64,32},{96,64},{128,96},{160,128},{192,160},{224,192},{33,... | collective-permute-start | bytes 460808 | tf_op jit(solution)/shard_map/ppermute | solution.py:23
  204.9 11.0 %collective-permute-start.10 = (f32[80,3,640]{2,0,1:T(8,128)S(1)}, f32[80,3,640]{2,0,1:T(8,128)S(1)}, u32[]{:S(2)}, u32[]{:S(2)}) collective-permute-start(f32[80,3,640]{2,0,1:T(8,128)S(1)} %get-tuple-element.10), channel_id=1, source_target_pairs={{0,1},{1,2},{2,3},{3,4},{4,5},{5,6},{6,7},{7,8},{8,9},{9,10},{10,1... | collective-permute-start | bytes 1843208 | tf_op jit(solution)/shard_map/ppermute | solution.py:21
  208.8 11.5 %collective-permute-start.11 = (f32[80,3,640]{2,0,1:T(8,128)S(1)}, f32[80,3,640]{2,0,1:T(8,128)S(1)}, u32[]{:S(2)}, u32[]{:S(2)}) collective-permute-start(f32[80,3,640]{2,0,1:T(8,128)S(1)} %get-tuple-element.11), channel_id=1, source_target_pairs={{1,0},{2,1},{3,2},{4,3},{5,4},{6,5},{7,6},{8,7},{9,8},{10,9},{11,1... | collective-permute-start | bytes 1843208 | tf_op jit(solution)/shard_map/ppermute | solution.py:23
where the time goes:
time: 281 us; the launch traced here: 279 us
  other arithmetic  152 us (54%)
  waiting for transfers between devices  47.6 us (17%)
  blocking collectives  40 us (14%)
  starting transfers between devices  35.2 us (13%)
  local copies, waits for them, and re-layouts  3.75 us (1%)
    add x6, other arithmetic, smear_valid(): result + kernel[offset] * lax.slice_in_dim(padded, offset, offset + lengt...  88.4 us
    reduce_max x3, other arithmetic, shards(): deviation = jnp.max(jnp.abs(blurred - 1.0))  45.5 us
    pmax x4, blocking collectives, over_axes(): value = lax.pmax(value, axis)  40 us
    ppermute x6, waiting for transfers between devices, with_halo(): lax.ppermute(head, axis, [((i + 1) % count, i) for i in range(ends)])  27 us
    ppermute x6, starting transfers between devices, with_halo(): lax.ppermute(tail, axis, [(i, (i + 1) % count) for i in range(ends)])  25.5 us
    ppermute x6, waiting for transfers between devices, with_halo(): lax.ppermute(tail, axis, [(i, (i + 1) % count) for i in range(ends)])  20.6 us
    ppermute x6, starting transfers between devices, with_halo(): lax.ppermute(head, axis, [((i + 1) % count, i) for i in range(ends)])  9.64 us
    mul x2, other arithmetic, shards(): product = weight * data_weight  8.77 us
  transfers between devices with their start and end apart: 12, of which 12 were waited for; matrix products, arithmetic and copies ran while one was open for 0% of the time, Pallas kernels for 0%

commit v1 on v0

v1 whole, which is shorter than its diff:
```python
import functools

import jax
import jax.numpy as jnp
from jax import lax
from jax.experimental import pallas as pl
from jax.experimental.pallas import tpu as pltpu
from jax.sharding import PartitionSpec as P

MESH = pl.DeviceIdType.MESH
F32 = jnp.float32
BF16 = jnp.bfloat16

NZ, NY, NX = 20, 80, 640
DEEP = 9
G = 4
ROWS = 96
XR = 104
Y_GROUPS = ((0, 7), (7, 11), (11, 15), (15, 20), (20, 23), (23, 27), (27, 29))
X_GROUPS = ((0, 20, 0, 24), (20, 23, 24, 8), (23, 27, 32, 8), (27, 29, 40, 8))
XS = 48
TINY = 1e-30
X_BLOCKS = ((0, 256, 0, 384), (256, 256, 128, 512), (512, 128, 384, 256))


def split(v):
    hi = v.astype(BF16)
    return hi, (v - hi.astype(F32)).astype(BF16)


def kernel(
    dw, taps, out, dev_out, p1, p2, p3, q, rh, rl, w0, w1, w2, ay, ob, stat, sx, rx,
    load_sem, out_sem, oss, osr, yss, ysr, xss, xsr, iss, isr,
):
    gy, gz = lax.axis_index("gy"), lax.axis_index("gz")
    ny, nz = lax.axis_size("gy"), lax.axis_size("gz")
    core = lax.rem(gz, 2)
    inner = gz + 1 - 2 * core
    outer = gz - 1 + 2 * core
    has_outer = jnp.logical_and(outer >= 0, outer < nz)
    has_up = gy < ny - 1
    has_down = gy > 0

    def plane(s):
        return core * s + (1 - core) * (NZ - 1 - s)

    loads = [
        pltpu.make_async_copy(dw.at[plane(s)], p1.at[s + 3, 0:NY], load_sem.at[s]) for s in range(NZ)
    ]
    for copy in loads:
        copy.start()

    barrier = pltpu.get_barrier_semaphore()
    pl.semaphore_signal(barrier, inc=1, device_id={"gz": inner}, device_id_type=MESH)

    @pl.when(has_outer)
    def _():
        pl.semaphore_signal(barrier, inc=1, device_id={"gz": outer}, device_id_type=MESH)

    @pl.when(has_up)
    def _():
        pl.semaphore_signal(barrier, inc=1, device_id={"gy": gy + 1}, device_id_type=MESH)

    @pl.when(has_down)
    def _():
        pl.semaphore_signal(barrier, inc=1, device_id={"gy": gy - 1}, device_id_type=MESH)

    p1[3:34, ROWS:XR, :] = jnp.zeros((31, XR - ROWS, NX), F32)
    p1[32:34, 0:ROWS, :] = jnp.zeros((2, ROWS, NX), F32)

    @pl.when(jnp.logical_not(has_up))
    def _():
        p1[3:32, 80:88, :] = jnp.zeros((29, 8, NX), F32)
        rx[1] = jnp.zeros((XS, NX), F32)

    @pl.when(jnp.logical_not(has_down))
    def _():
        p1[3:32, 88:96, :] = jnp.zeros((29, 8, NX), F32)
        rx[0] = jnp.zeros((XS, NX), F32)

    @pl.when(jnp.logical_not(has_outer))
    def _():
        def clear(i, carry):
            p1[23 + i, 0:ROWS, :] = jnp.zeros((ROWS, NX), F32)
            return carry

        lax.fori_loop(0, DEEP, clear, 0)
        rx[0, 24:XS, :] = jnp.zeros((XS - 24, NX), F32)
        rx[1, 24:XS, :] = jnp.zeros((XS - 24, NX), F32)

    pl.semaphore_wait(
        barrier, 1 + has_outer.astype(jnp.int32) + has_up.astype(jnp.int32) + has_down.astype(jnp.int32)
    )

    def remote(src, dst, ss, rs, where):
        return pltpu.make_async_remote_copy(
            src_ref=src, dst_ref=dst, send_sem=ss, recv_sem=rs, device_id=where, device_id_type=MESH
        )

    outs = [
        remote(dw.at[plane(19 - i)], p1.at[23 + i, 0:NY], oss.at[i], osr.at[i], {"gz": outer})
        for i in range(DEEP)
    ]

    @pl.when(has_outer)
    def _():
        for copy in outs:
            copy.start()

    inner_own = [
        remote(dw.at[plane(i)], p1.at[2 - i, 0:NY], iss.at[i], isr.at[i], {"gz": inner}) for i in range(3)
    ]
    for copy in inner_own:
        copy.start()

    def y_copies(n):
        a, b = Y_GROUPS[n]
        pa, pb = a + 3, b + 3
        up = remote(p1.at[pa:pb, 72:80], p1.at[pa:pb, 88:96], yss.at[0, n], ysr.at[0, n], {"gy": gy + 1})
        down = remote(p1.at[pa:pb, 0:8], p1.at[pa:pb, 80:88], yss.at[1, n], ysr.at[1, n], {"gy": gy - 1})
        return up, down

    def x_copies(n):
        _, _, slot, size = X_GROUPS[n]
        at = slice(slot, slot + size)
        up = remote(sx.at[0, at], rx.at[0, at], xss.at[0, n], xsr.at[0, n], {"gy": gy + 1})
        down = remote(sx.at[1, at], rx.at[1, at], xss.at[1, n], xsr.at[1, n], {"gy": gy - 1})
        return up, down

    def start_y(n):
        up, down = y_copies(n)

        @pl.when(has_up)
        def _():
            up.start()

        @pl.when(has_down)
        def _():
            down.start()

    def start_x(n):
        a, b, slot, size = X_GROUPS[n]
        for i in range(size):
            s = min(a + i, b - 1)
            sx[0, slot + i : slot + i + 1, :] = p1[s + 3, 71:72, :]
            sx[1, slot + i : slot + i + 1, :] = p1[s + 3, 8:9, :]
        up, down = x_copies(n)

        @pl.when(has_up)
        def _():
            up.start()

        @pl.when(has_down)
        def _():
            down.start()

    def wait_y(n):
        up, down = y_copies(n)

        @pl.when(has_down)
        def _():
            up.wait_recv()

        @pl.when(has_up)
        def _():
            down.wait_recv()

    def wait_x(n):
        up, down = x_copies(n)

        @pl.when(has_down)
        def _():
            up.wait_recv()

        @pl.when(has_up)
        def _():
            down.wait_recv()

        a, b, slot, size = X_GROUPS[n]
        for i in range(b - a):
            p1[a + i + 3, 96:97, :] = rx[0, slot + i : slot + i + 1, :]
            p1[a + i + 3, 97:98, :] = rx[1, slot + i : slot + i + 1, :]

    for n in range(4):
        for s in range(*Y_GROUPS[n]):
            loads[s].wait()
        start_y(n)
    start_x(0)

    tv = taps[...]
    tv = tv / jnp.sum(tv, axis=1, keepdims=True)
    flip = core == 0
    kz = [jnp.where(flip, tv[1:2, 6 - k : 7 - k], tv[1:2, k : k + 1]) for k in range(7)]

    i = lax.broadcasted_iota(jnp.int32, (128, 128), 0)
    j = lax.broadcasted_iota(jnp.int32, (128, 128), 1)
    blocks = {}
    for delta in (-1, 0, 1):
        diff = delta * 128 + i - j + 3
        t = jnp.zeros((128, 128), F32)
        for k in range(7):
            t = jnp.where(diff == k, tv[2:3, k : k + 1], t)
        blocks[delta] = split(t)
    zero = jnp.zeros((128, 128), BF16)
    for w, (n0, nn, k0, kn) in zip((w0, w1, w2), X_BLOCKS):
        for part in range(3):
            for kb in range(kn // 128):
                for nb in range(nn // 128):
                    delta = (k0 // 128 + kb) - (n0 // 128 + nb)
                    block = blocks[delta][1 if part == 2 else 0] if abs(delta) <= 1 else zero
                    w[part * kn + kb * 128 : part * kn + (kb + 1) * 128, nb * 128 : (nb + 1) * 128] = block

    o = lax.broadcasted_iota(jnp.int32, (ROWS, 128), 0)
    i = lax.broadcasted_iota(jnp.int32, (ROWS, 128), 1)
    yo = jnp.where(o < 88, o, o - 96)
    yi = jnp.where(i < 88, i, jnp.where(i < 96, i - 96, jnp.where(i == 96, -9, jnp.where(i == 97, 88, 4096))))
    diff = yi - yo + 3
    t = jnp.zeros((ROWS, 128), F32)
    for k in range(7):
        t = jnp.where(diff == k, tv[0:1, k : k + 1], t)
    t_hi, t_lo = split(t)
    ay[0:ROWS, 0:128] = t_hi
    ay[0:ROWS, 128:256] = t_hi
    ay[ROWS : 2 * ROWS, 0:128] = t_lo
    ay[ROWS : 2 * ROWS, 128:256] = jnp.zeros((ROWS, 128), BF16)

    for g in range(G):
        q[g, 96:128, :] = jnp.zeros((32, NX), BF16)
        q[g, 224:256, :] = jnp.zeros((32, NX), BF16)
    for t in range(3):
        stat[t, 0] = jnp.zeros((8, 128), F32)
        stat[t, 1] = jnp.full((8, 128), 3e38, F32)

    def chunk(t, d):
        src = (p1, p2, p3)[t]
        base = d * G
        strips = 7 if t == 0 else 6
        for strip in range(strips):
            r0 = strip * 16
            height = 8 if strip == 6 else 16
            for lb in range(5):
                lanes = slice(lb * 128, (lb + 1) * 128)
                p = [src[base + k, r0 : r0 + height, lanes] for k in range(G + 6)]
                for g in range(G):
                    acc = kz[0] * p[g]
                    for k in range(1, 7):
                        acc = acc + kz[k] * p[g + k]
                    if height == 8:
                        acc = jnp.concatenate([acc, jnp.zeros((8, 128), F32)], axis=0)
                    hi, lo = split(acc)
                    q[g, r0 : r0 + 16, lanes] = hi
                    q[g, 128 + r0 : 144 + r0, lanes] = lo
        rows = 80 if t == 2 else ROWS
        for g in range(G):
            if t == 2:
                y = jnp.dot(ay[0:80, :], q[g], preferred_element_type=F32) + jnp.dot(
                    ay[ROWS : ROWS + 80, :], q[g], preferred_element_type=F32
                )
            else:
                y = jnp.dot(ay[...], q[g], preferred_element_type=F32)
                y = y[0:ROWS] + y[ROWS : 2 * ROWS]
            hi, lo = split(y)
            rh[g * rows : (g + 1) * rows, :] = hi
            rl[g * rows : (g + 1) * rows, :] = lo
        m = G * rows
        top = jnp.zeros((8, 128), F32)
        low = jnp.full((8, 128), 3e38, F32)
        for w, (n0, nn, k0, kn) in zip((w0, w1, w2), X_BLOCKS):
            hi, lo = rh[0:m, k0 : k0 + kn], rl[0:m, k0 : k0 + kn]
            b = jnp.dot(jnp.concatenate([hi, lo, hi], axis=1), w[...], preferred_element_type=F32)
            for g in range(G):
                for r0 in range(0, rows, 16):
                    for lb in range(nn // 128):
                        v = b[g * rows + r0 : g * rows + r0 + 16, lb * 128 : (lb + 1) * 128]
                        lanes = slice(n0 + lb * 128, n0 + (lb + 1) * 128)
                        if r0 < 80:
                            top = jnp.maximum(top, jnp.maximum(v[0:8], v[8:16]))
                            low = jnp.minimum(low, jnp.minimum(v[0:8], v[8:16]))
                        p = src[base + 3 + g, r0 : r0 + 16, lanes]
                        if t == 2:
                            f = p1[base + 3 + g, r0 : r0 + 16, lanes]
                            ob[base + g, r0 : r0 + 16, lanes] = p / (v * f)
                        else:
                            dst = (p2, p3)[t]
                            dst[base + 3 + g, r0 : r0 + 16, lanes] = p / jnp.maximum(v, TINY)
        own = d * G < NZ
        stat[t, 0] = jnp.where(own, jnp.maximum(stat[t, 0], top), stat[t, 0])
        stat[t, 1] = jnp.where(own, jnp.minimum(stat[t, 1], low), stat[t, 1])

    inner_rim = [
        remote(p1.at[3 + i, NY:XR], p1.at[2 - i, NY:XR], iss.at[3 + i], isr.at[3 + i], {"gz": inner})
        for i in range(3)
    ]
    inner_p2 = [
        remote(p2.at[3 + i], p2.at[2 - i], iss.at[6 + i], isr.at[6 + i], {"gz": inner}) for i in range(3)
    ]
    inner_p3 = [
        remote(p3.at[3 + i], p3.at[2 - i], iss.at[9 + i], isr.at[9 + i], {"gz": inner}) for i in range(3)
    ]
    outputs = lambda c: [
        pltpu.make_async_copy(ob.at[c * G + g], out.at[plane(c * G + g)], out_sem.at[c * G + g]) for g in range(G)
    ]

    def forward(n):
        a, b = Y_GROUPS[n]
        for s in range(a, b):
            outs[s - 20].wait_recv()
        start_y(n)
        start_x(n - 3)

    def wave(d, carry):
        @pl.when(d == 0)
        def _():
            wait_x(0)
            wait_y(0)
            for copy in inner_rim:
                copy.start()
            for copy in inner_own + inner_rim:
                copy.wait_recv()

        for n in (1, 2, 3):

            @pl.when(d == n)
            def _(n=n):
                wait_y(n)

        for n in (4, 5, 6):

            @pl.when(jnp.logical_and(d == n, has_outer))
            def _(n=n):
                wait_y(n)
                wait_x(n - 3)

        chunk(0, d)

        @pl.when(d == 0)
        def _():
            for copy in inner_p2:
                copy.start()

        for n in (4, 5, 6):

            @pl.when(jnp.logical_and(d == n - 1, has_outer))
            def _(n=n):
                forward(n)

        @pl.when(d == 1)
        def _():
            for copy in inner_p2:
                copy.wait_recv()

        @pl.when(d >= 1)
        def _():
            chunk(1, d - 1)

        @pl.when(d == 1)
        def _():
            for copy in inner_p3:
                copy.start()

        @pl.when(d == 2)
        def _():
            for copy in inner_p3:
                copy.wait_recv()

        @pl.when(d >= 2)
        def _():
            chunk(2, d - 2)
            for g in range(G):
                s = (d - 2) * G + g
                pltpu.make_async_copy(ob.at[s], out.at[plane(s)], out_sem.at[s]).start()

        return carry

    lax.fori_loop(0, 7, wave, 0)

    row = lax.broadcasted_iota(jnp.int32, (8, 128), 0)
    dev = jnp.zeros((8, 128), F32)
    for t in range(3):
        worst = jnp.maximum(jnp.max(stat[t, 0]) - 1.0, 1.0 - jnp.min(stat[t, 1]))
        dev = jnp.where(row == t, worst, dev)
    dev_out[...] = dev

    for s in range(NZ):
        pltpu.make_async_copy(ob.at[s], out.at[plane(s)], out_sem.at[s]).wait()
    for copy in inner_own + inner_rim + inner_p2 + inner_p3:
        copy.wait_send()

    @pl.when(has_outer)
    def _():
        for copy in outs:
            copy.wait_send()

    def sent(copies):
        up, down = copies

        @pl.when(has_up)
        def _():
            up.wait_send()

        @pl.when(has_down)
        def _():
            down.wait_send()

    for n in range(4):
        sent(y_copies(n))
    sent(x_copies(0))

    @pl.when(has_outer)
    def _():
        for n in (4, 5, 6):
            sent(y_copies(n))
            sent(x_copies(n - 3))


def shards(data_weight, blob_taps):
    dma = pltpu.SemaphoreType.DMA
    weight, dev = pl.pallas_call(
        kernel,
        out_shape=(
            jax.ShapeDtypeStruct((NZ, NY, NX), F32),
            jax.ShapeDtypeStruct((8, 128), F32),
        ),
        in_specs=[pl.BlockSpec(memory_space=pl.ANY), pl.BlockSpec(memory_space=pltpu.VMEM)],
        out_specs=(pl.BlockSpec(memory_space=pl.ANY), pl.BlockSpec(memory_space=pltpu.VMEM)),
        scratch_shapes=[
            pltpu.VMEM((34, XR, NX), F32),
            pltpu.VMEM((31, ROWS, NX), F32),
            pltpu.VMEM((27, ROWS, NX), F32),
            pltpu.VMEM((G, 256, NX), BF16),
            pltpu.VMEM((G * ROWS, NX), BF16),
            pltpu.VMEM((G * ROWS, NX), BF16),
            pltpu.VMEM((3 * 384, 256), BF16),
            pltpu.VMEM((3 * 512, 256), BF16),
            pltpu.VMEM((3 * 256, 128), BF16),
            pltpu.VMEM((2 * ROWS, 256), BF16),
            pltpu.VMEM((NZ, NY, NX), F32),
            pltpu.VMEM((3, 2, 8, 128), F32),
            pltpu.VMEM((2, XS, NX), F32),
            pltpu.VMEM((2, XS, NX), F32),
            dma((NZ,)),
            dma((NZ,)),
            dma((DEEP,)),
            dma((DEEP,)),
            dma((2, 7)),
            dma((2, 7)),
            dma((2, 4)),
            dma((2, 4)),
            dma((12,)),
            dma((12,)),
        ],
        compiler_params=pltpu.CompilerParams(
            collective_id=0, has_side_effects=True, vmem_limit_bytes=60 * 1024 * 1024
        ),
    )(jnp.transpose(data_weight, (1, 0, 2)), blob_taps)
    changes = lax.pmax(dev[:3, 0], ("gy", "gz"))
    return jnp.transpose(weight, (1, 0, 2)), changes


def solution(mesh):
    return jax.shard_map(
        shards,
        mesh=mesh,
        in_specs=(P("gy", "gz", None), P()),
        out_specs=(P("gy", "gz", None), P()),
        check_vma=False,
    )
```

time: 281 us -> 140 us (0.50)
  other arithmetic: 152 us -> 0 us
  Pallas kernels: 0 us -> 55.8 us
  waiting for transfers between devices: 47.6 us -> 0 us
  blocking collectives: 40 us -> 78.5 us
  starting transfers between devices: 35.2 us -> 0 us
    add x6 -> x0, other arithmetic: 88.4 us -> none  [smear_valid(): result + kernel[offset] * lax.slice_in_dim(padded, offset, offset + lengt...]
    pallas_call x0 -> x1, Pallas kernels: none -> 55.8 us  [shards(): pl.pallas_call(kernel, out_shape=(jax.ShapeDtypeStruct((NZ, NY, NX), F32)...]
    ppermute x12 -> x0, waiting for transfers between devices: 47.6 us -> none  [the longest x6 27 us: with_halo(): lax.ppermute(head, axis, [((i + 1) % count, i) for i in range(ends)])]
    reduce_max x3 -> x0, other arithmetic: 45.5 us -> none  [shards(): deviation = jnp.max(jnp.abs(blurred - 1.0))]
    pmax x4 -> x1, blocking collectives: 40 us -> 78.5 us  [shards(): changes = lax.pmax(dev[:3, 0], ('gy', 'gz'))]
    ppermute x12 -> x0, starting transfers between devices: 35.2 us -> none  [the longest x6 25.5 us: with_halo(): lax.ppermute(tail, axis, [(i, (i + 1) % count) for i in range(ends)])]
    mul x2 -> x0, other arithmetic: 8.77 us -> none  [shards(): product = weight * data_weight]
    div x2 -> x0, other arithmetic: 6.67 us -> none  [the longest x1 5.92 us: shards(): weight = weight / blurred]
  transfers between devices with their start and end apart: 12 -> 0, of which waited for: 12 -> 0; matrix products, arithmetic and copies ran while one was open for 0% -> 0% of each run, Pallas kernels for 0% -> 0%
where the time goes in v1:
time: 140 us
  blocking collectives  78.5 us (56%)
  Pallas kernels  55.8 us (40%)
  local copies, waits for them, and re-layouts  5.19 us (4%)
    pmax x1, blocking collectives, shards(): changes = lax.pmax(dev[:3, 0], ('gy', 'gz'))  78.5 us
    pallas_call x1, Pallas kernels, shards(): pl.pallas_call(kernel, out_shape=(jax.ShapeDtypeStruct((NZ, NY, NX), F32)...  55.8 us
    unnamed x1, local copies, waits for them, and re-layouts  4.4 us

profile of v1, /device:TPU:1, one launch (start us, length us, event | category | flops | bytes accessed | tf_op | source)
XLA Modules:
  0.0 140.1 jit_solution(7731680514985951550)
XLA Ops:
  0.6 55.8 %shard_map.41 = (f32[20,80,640]{2,1,0:T(8,128)}, f32[8,128]{1,0:T(8,128)}) custom-call(f32[20,80,640]{2,1,0:T(8,128)} %bitcast.2, f32[3,7]{1,0:T(4,128)} %taps.1), custom_call_target="tpu_custom_call" | custom-call | tf_op jit(solution)/shard_map/pallas_call | solution.py:418
  56.4 0.8 slice_reduce_fusion
  57.2 78.5 %pmax.7 = f32[3]{0:T(128)} all-reduce(f32[3]{0:T(128)S(1)} %slice_reduce_fusion), channel_id=1, replica_groups=mesh['gy'=8,'gz'=32] {'gy','gz'}, use_global_device_ids=true, to_apply=%region_0.0 | all-reduce | flops 3 | bytes 24 | tf_op jit(solution)/shard_map/pmax | solution.py:456
  135.7 4.4 %copy.5 = f32[80,20,640]{2,0,1:T(8,128)} copy(f32[80,20,640]{2,0,1:T(8,128)} %bitcast.3) | data formatting | bytes 8192000

commit v2 on v1

--- a/solution.py
+++ b/solution.py
@@ -20,6 +20,7 @@
 X_GROUPS = ((0, 20, 0, 24), (20, 23, 24, 8), (23, 27, 32, 8), (27, 29, 40, 8))
 XS = 48
 TINY = 1e-30
+REDUCE = ((8, 1, "gz"), (4, 8, "gz"), (8, 1, "gy"))
 X_BLOCKS = ((0, 256, 0, 384), (256, 256, 128, 512), (512, 128, 384, 256))
 
 
@@ -29,8 +30,9 @@
 
 
 def kernel(
-    dw, taps, out, dev_out, p1, p2, p3, q, rh, rl, w0, w1, w2, ay, ob, stat, sx, rx,
-    load_sem, out_sem, oss, osr, yss, ysr, xss, xsr, iss, isr,
+    dw, taps, out, dev_out, p1, p2, p3, q, rh, rl, w0, w1, w2, ay, stat, sx, rx,
+    mine, seen,
+    load_sem, oss, osr, yss, ysr, xss, xsr, iss, isr, rds, rdr, met_z, met_y,
 ):
     gy, gz = lax.axis_index("gy"), lax.axis_index("gz")
     ny, nz = lax.axis_size("gy"), lax.axis_size("gz")
@@ -51,19 +53,9 @@
         copy.start()
 
     barrier = pltpu.get_barrier_semaphore()
-    pl.semaphore_signal(barrier, inc=1, device_id={"gz": inner}, device_id_type=MESH)
-
-    @pl.when(has_outer)
-    def _():
-        pl.semaphore_signal(barrier, inc=1, device_id={"gz": outer}, device_id_type=MESH)
-
-    @pl.when(has_up)
-    def _():
-        pl.semaphore_signal(barrier, inc=1, device_id={"gy": gy + 1}, device_id_type=MESH)
-
-    @pl.when(has_down)
-    def _():
-        pl.semaphore_signal(barrier, inc=1, device_id={"gy": gy - 1}, device_id_type=MESH)
+    for axis, me, size in (("gz", gz, nz), ("gy", gy, ny)):
+        for far in (1, size - 1):
+            pl.semaphore_signal(barrier, inc=1, device_id={axis: lax.rem(me + far, size)}, device_id_type=MESH)
 
     p1[3:34, ROWS:XR, :] = jnp.zeros((31, XR - ROWS, NX), F32)
     p1[32:34, 0:ROWS, :] = jnp.zeros((2, ROWS, NX), F32)
@@ -88,9 +80,7 @@
         rx[0, 24:XS, :] = jnp.zeros((XS - 24, NX), F32)
         rx[1, 24:XS, :] = jnp.zeros((XS - 24, NX), F32)
 
-    pl.semaphore_wait(
-        barrier, 1 + has_outer.astype(jnp.int32) + has_up.astype(jnp.int32) + has_down.astype(jnp.int32)
-    )
+    pl.semaphore_wait(barrier, 4)
 
     def remote(src, dst, ss, rs, where):
         return pltpu.make_async_remote_copy(
@@ -279,7 +269,7 @@
                         p = src[base + 3 + g, r0 : r0 + 16, lanes]
                         if t == 2:
                             f = p1[base + 3 + g, r0 : r0 + 16, lanes]
-                            ob[base + g, r0 : r0 + 16, lanes] = p / (v * f)
+                            out[plane(base + g), r0 : r0 + 16, lanes] = p / (v * f)
                         else:
                             dst = (p2, p3)[t]
                             dst[base + 3 + g, r0 : r0 + 16, lanes] = p / jnp.maximum(v, TINY)
@@ -297,10 +287,6 @@
     inner_p3 = [
         remote(p3.at[3 + i], p3.at[2 - i], iss.at[9 + i], isr.at[9 + i], {"gz": inner}) for i in range(3)
     ]
-    outputs = lambda c: [
-        pltpu.make_async_copy(ob.at[c * G + g], out.at[plane(c * G + g)], out_sem.at[c * G + g]) for g in range(G)
-    ]
-
     def forward(n):
         a, b = Y_GROUPS[n]
         for s in range(a, b):
@@ -308,7 +294,29 @@
         start_y(n)
         start_x(n - 3)
 
+    def meet(k, wait):
+        far = 2**k
+        for axis, me, size in (("gz", gz, nz), ("gy", gy, ny)):
+            if 4 * far <= size:
+                sem = (met_z if axis == "gz" else met_y).at[k]
+                if wait:
+                    pl.semaphore_wait(sem, 2)
+                else:
+                    for by in (far, size - far):
+                        pl.semaphore_signal(
+                            sem, inc=1, device_id={axis: lax.rem(me + by, size)}, device_id_type=MESH
+                        )
+
     def wave(d, carry):
+        for k in range(5):
+
+            @pl.when(d == k)
+            def _(k=k):
+                if k > 0:
+                    meet(k - 1, True)
+                if k < 4:
+                    meet(k, False)
+
         @pl.when(d == 0)
         def _():
             wait_x(0)
@@ -366,23 +374,55 @@
         @pl.when(d >= 2)
         def _():
             chunk(2, d - 2)
-            for g in range(G):
-                s = (d - 2) * G + g
-                pltpu.make_async_copy(ob.at[s], out.at[plane(s)], out_sem.at[s]).start()
 
         return carry
 
     lax.fori_loop(0, 7, wave, 0)
 
-    row = lax.broadcasted_iota(jnp.int32, (8, 128), 0)
-    dev = jnp.zeros((8, 128), F32)
+    lane = lax.broadcasted_iota(jnp.int32, (1, 128), 1)
+    dev = jnp.zeros((1, 128), F32)
     for t in range(3):
         worst = jnp.maximum(jnp.max(stat[t, 0]) - 1.0, 1.0 - jnp.min(stat[t, 1]))
-        dev = jnp.where(row == t, worst, dev)
+        dev = jnp.where(lane == t, worst, dev)
+
+    value = dev
+    for stage, (size, stride, axis) in enumerate(REDUCE):
+        me = gy if axis == "gy" else gz
+        member = lax.rem(me // stride, size)
+        seen[stage, member] = value
+        mine[stage] = value
+
+        def copy(k):
+            other = lax.rem(member + k, size)
+            return remote(
+                mine.at[stage], seen.at[stage, member], rds.at[stage, k], rdr.at[stage, member],
+                {axis: me + (other - member) * stride},
+            )
+
+        def arrival(k):
+            other = lax.rem(member + k, size)
+            return remote(
+                mine.at[stage], seen.at[stage, other], rds.at[stage, k], rdr.at[stage, other],
+                {axis: me + (other - member) * stride},
+            )
+
+        for k in range(1, size):
+            copy(k).start()
+        for k in range(1, size):
+            arrival(k).wait_recv()
+        value = jnp.max(seen[stage, 0:size], axis=0)
+    for stage, (size, stride, axis) in enumerate(REDUCE):
+        me = gy if axis == "gy" else gz
+        member = lax.rem(me // stride, size)
+        for k in range(1, size):
+            other = lax.rem(member + k, size)
+            remote(
+                mine.at[stage], seen.at[stage, member], rds.at[stage, k], rdr.at[stage, member],
+                {axis: me + (other - member) * stride},
+            ).wait_send()
+    dev = value
     dev_out[...] = dev
 
-    for s in range(NZ):
-        pltpu.make_async_copy(ob.at[s], out.at[plane(s)], out_sem.at[s]).wait()
     for copy in inner_own + inner_rim + inner_p2 + inner_p3:
         copy.wait_send()
 
@@ -419,10 +459,10 @@
         kernel,
         out_shape=(
             jax.ShapeDtypeStruct((NZ, NY, NX), F32),
-            jax.ShapeDtypeStruct((8, 128), F32),
+            jax.ShapeDtypeStruct((1, 128), F32),
         ),
         in_specs=[pl.BlockSpec(memory_space=pl.ANY), pl.BlockSpec(memory_space=pltpu.VMEM)],
-        out_specs=(pl.BlockSpec(memory_space=pl.ANY), pl.BlockSpec(memory_space=pltpu.VMEM)),
+        out_specs=(pl.BlockSpec(memory_space=pltpu.VMEM), pl.BlockSpec(memory_space=pltpu.VMEM)),
         scratch_shapes=[
             pltpu.VMEM((34, XR, NX), F32),
             pltpu.VMEM((31, ROWS, NX), F32),
@@ -434,11 +474,11 @@
             pltpu.VMEM((3 * 512, 256), BF16),
             pltpu.VMEM((3 * 256, 128), BF16),
             pltpu.VMEM((2 * ROWS, 256), BF16),
-            pltpu.VMEM((NZ, NY, NX), F32),
             pltpu.VMEM((3, 2, 8, 128), F32),
             pltpu.VMEM((2, XS, NX), F32),
             pltpu.VMEM((2, XS, NX), F32),
-            dma((NZ,)),
+            pltpu.VMEM((len(REDUCE), 1, 128), F32),
+            pltpu.VMEM((len(REDUCE), 8, 1, 128), F32),
             dma((NZ,)),
             dma((DEEP,)),
             dma((DEEP,)),
@@ -448,13 +488,16 @@
             dma((2, 4)),
             dma((12,)),
             dma((12,)),
+            dma((len(REDUCE), 8)),
+            dma((len(REDUCE), 8)),
+            pltpu.SemaphoreType.REGULAR((4,)),
+            pltpu.SemaphoreType.REGULAR((2,)),
         ],
         compiler_params=pltpu.CompilerParams(
-            collective_id=0, has_side_effects=True, vmem_limit_bytes=60 * 1024 * 1024
+            collective_id=0, has_side_effects=True, vmem_limit_bytes=50 * 1024 * 1024
         ),
     )(jnp.transpose(data_weight, (1, 0, 2)), blob_taps)
-    changes = lax.pmax(dev[:3, 0], ("gy", "gz"))
-    return jnp.transpose(weight, (1, 0, 2)), changes
+    return jnp.transpose(weight, (1, 0, 2)), dev[0, :3]
 
 
 def solution(mesh):

time: 140 us -> 74.2 us (0.53)
  blocking collectives: 78.5 us -> 0 us
  Pallas kernels: 55.8 us -> 70.2 us
  local copies, waits for them, and re-layouts: 5.19 us -> 3.16 us
    pmax x1 -> x0, blocking collectives: 78.5 us -> none  [shards(): changes = lax.pmax(dev[:3, 0], ('gy', 'gz'))]
    pallas_call x1, Pallas kernels: 55.8 us -> 70.2 us  [shards(): pl.pallas_call(kernel, out_shape=(jax.ShapeDtypeStruct((NZ, NY, NX), F32)...]
    unnamed x1 -> x3, local copies, waits for them, and re-layouts: 4.4 us -> 2.65 us
where the time goes in v2:
time: 74.2 us; the launch traced here: 74 us
  Pallas kernels  70.2 us (95%)
  local copies, waits for them, and re-layouts  3.16 us (4%)
    pallas_call x1, Pallas kernels, shards(): pl.pallas_call(kernel, out_shape=(jax.ShapeDtypeStruct((NZ, NY, NX), F32)...  70.2 us
    unnamed x3, local copies, waits for them, and re-layouts  2.65 us

profile of v2, /device:TPU:1, one launch (start us, length us, event | category | flops | bytes accessed | tf_op | source)
XLA Modules:
  0.0 74.0 jit_solution(13050435547444429019)
XLA Ops:
  0.6 0.0 copy-start
  0.6 0.7 copy-done
  1.3 70.2 %shard_map.41 = (f32[20,80,640]{2,1,0:T(8,128)S(1)}, f32[1,128]{1,0:T(1,128)S(1)}) custom-call(f32[20,80,640]{2,1,0:T(8,128)} %bitcast.5, f32[3,7]{1,0:T(4,128)S(1)} %copy-done), custom_call_target="tpu_custom_call" | custom-call | tf_op jit(solution)/shard_map/pallas_call | solution.py:458
  71.5 0.5 slice_bitcast_fusion
  72.1 2.0 %copy.5 = f32[80,20,640]{2,0,1:T(8,128)} copy(f32[80,20,640]{2,0,1:T(8,128)S(1)} %bitcast.4) | data formatting | bytes 8192000
Async XLA Ops:
  0.6 0.7 copy-start

commit v3 on v2

--- a/solution.py
+++ b/solution.py
@@ -17,11 +17,11 @@
 ROWS = 96
 XR = 104
 Y_GROUPS = ((0, 7), (7, 11), (11, 15), (15, 20), (20, 23), (23, 27), (27, 29))
-X_GROUPS = ((0, 20, 0, 24), (20, 23, 24, 8), (23, 27, 32, 8), (27, 29, 40, 8))
+X_GROUPS = ((0, 7, 0, 8), (7, 20, 8, 16), (20, 23, 24, 8), (23, 27, 32, 8), (27, 29, 40, 8))
 XS = 48
 TINY = 1e-30
-REDUCE = ((8, 1, "gz"), (4, 8, "gz"), (8, 1, "gy"))
-X_BLOCKS = ((0, 256, 0, 384), (256, 256, 128, 512), (512, 128, 384, 256))
+REDUCE = ((32, 1, "gz"), (8, 1, "gy"))
+X_BLOCKS = ((0, 256, 0), (256, 256, 1), (512, 128, 0))
 
 
 def split(v):
@@ -30,7 +30,7 @@
 
 
 def kernel(
-    dw, taps, out, dev_out, p1, p2, p3, q, rh, rl, w0, w1, w2, ay, stat, sx, rx,
+    dw, taps, out, dev_out, p1, p2, p3, q, rh, rl, edge, w0, w1, w2, ay, stat, sx, rx,
     mine, seen,
     load_sem, oss, osr, yss, ysr, xss, xsr, iss, isr, rds, rdr, met_z, met_y,
 ):
@@ -92,17 +92,9 @@
         for i in range(DEEP)
     ]
 
-    @pl.when(has_outer)
-    def _():
-        for copy in outs:
-            copy.start()
-
     inner_own = [
         remote(dw.at[plane(i)], p1.at[2 - i, 0:NY], iss.at[i], isr.at[i], {"gz": inner}) for i in range(3)
     ]
-    for copy in inner_own:
-        copy.start()
-
     def y_copies(n):
         a, b = Y_GROUPS[n]
         pa, pb = a + 3, b + 3
@@ -171,34 +163,56 @@
             p1[a + i + 3, 96:97, :] = rx[0, slot + i : slot + i + 1, :]
             p1[a + i + 3, 97:98, :] = rx[1, slot + i : slot + i + 1, :]
 
-    for n in range(4):
-        for s in range(*Y_GROUPS[n]):
-            loads[s].wait()
-        start_y(n)
+    for s in range(7):
+        loads[s].wait()
     start_x(0)
+    start_y(0)
+
+    @pl.when(has_outer)
+    def _():
+        for copy in outs:
+            copy.start()
+
+    for copy in inner_own:
+        copy.start()
+
+    for s in range(7, NZ):
+        loads[s].wait()
+    start_y(1)
+    start_x(1)
+    start_y(2)
+    start_y(3)
 
     tv = taps[...]
     tv = tv / jnp.sum(tv, axis=1, keepdims=True)
     flip = core == 0
     kz = [jnp.where(flip, tv[1:2, 6 - k : 7 - k], tv[1:2, k : k + 1]) for k in range(7)]
 
+    def banded(diff):
+        t = jnp.zeros(diff.shape, F32)
+        for k in range(7):
+            t = jnp.where(diff == k - 3, tv[2:3, k : k + 1], t)
+        return split(t)
+
     i = lax.broadcasted_iota(jnp.int32, (128, 128), 0)
     j = lax.broadcasted_iota(jnp.int32, (128, 128), 1)
-    blocks = {}
-    for delta in (-1, 0, 1):
-        diff = delta * 128 + i - j + 3
-        t = jnp.zeros((128, 128), F32)
-        for k in range(7):
-            t = jnp.where(diff == k, tv[2:3, k : k + 1], t)
-        blocks[delta] = split(t)
-    zero = jnp.zeros((128, 128), BF16)
-    for w, (n0, nn, k0, kn) in zip((w0, w1, w2), X_BLOCKS):
+    blocks = [banded(delta * 128 + i - j) for delta in (-1, 0, 1)]
+    for w, (n0, nn, _) in zip((w0, w1, w2), X_BLOCKS):
         for part in range(3):
-            for kb in range(kn // 128):
+            for kb in range(nn // 128):
                 for nb in range(nn // 128):
-                    delta = (k0 // 128 + kb) - (n0 // 128 + nb)
-                    block = blocks[delta][1 if part == 2 else 0] if abs(delta) <= 1 else zero
-                    w[part * kn + kb * 128 : part * kn + (kb + 1) * 128, nb * 128 : (nb + 1) * 128] = block
+                    rows = slice(part * nn + kb * 128, part * nn + (kb + 1) * 128)
+                    w[rows, nb * 128 : (nb + 1) * 128] = blocks[kb - nb + 1][part // 2]
+        part = jnp.where(jnp.logical_or(i < 3, i >= 125), 0, jnp.where(i < 11, 1, 2))
+        step = i - 8 * part
+        step = jnp.where(step >= 125, step - 128, step)
+        right = jnp.logical_and(step >= 0, step < (3 if n0 + nn < NX else 0))
+        left = jnp.logical_and(step < 0, step >= (-3 if n0 > 0 else 0))
+        for nb in range(nn // 128):
+            out_lane = j + nb * 128
+            diff = jnp.where(right, nn + step - out_lane, jnp.where(left, step - out_lane, 4096))
+            hi, lo = banded(diff)
+            w[3 * nn : 3 * nn + 128, nb * 128 : (nb + 1) * 128] = jnp.where(part == 2, lo.astype(F32), hi.astype(F32)).astype(BF16)
 
     o = lax.broadcasted_iota(jnp.int32, (ROWS, 128), 0)
     i = lax.broadcasted_iota(jnp.int32, (ROWS, 128), 1)
@@ -250,14 +264,27 @@
                 y = jnp.dot(ay[...], q[g], preferred_element_type=F32)
                 y = y[0:ROWS] + y[ROWS : 2 * ROWS]
             hi, lo = split(y)
-            rh[g * rows : (g + 1) * rows, :] = hi
-            rl[g * rows : (g + 1) * rows, :] = lo
+            at = slice(g * rows, (g + 1) * rows)
+            rh[at, :] = hi
+            rl[at, :] = lo
+            lane = lax.broadcasted_iota(jnp.int32, (rows, 128), 1)
+            for e, (after, ahead) in enumerate(((2, 3), (4, 1))):
+                rim = jnp.where(
+                    lane < 64, y[:, after * 128 : (after + 1) * 128], y[:, ahead * 128 : (ahead + 1) * 128]
+                )
+                rim_hi = rim.astype(BF16).astype(F32)
+                rim = jnp.where(
+                    jnp.logical_or(lane < 3, lane >= 125),
+                    rim_hi,
+                    jnp.where(lane < 11, pltpu.roll(rim - rim_hi, 8, 1), pltpu.roll(rim_hi, 16, 1)),
+                )
+                edge[e, at, :] = rim.astype(BF16)
         m = G * rows
         top = jnp.zeros((8, 128), F32)
         low = jnp.full((8, 128), 3e38, F32)
-        for w, (n0, nn, k0, kn) in zip((w0, w1, w2), X_BLOCKS):
-            hi, lo = rh[0:m, k0 : k0 + kn], rl[0:m, k0 : k0 + kn]
-            b = jnp.dot(jnp.concatenate([hi, lo, hi], axis=1), w[...], preferred_element_type=F32)
+        for w, (n0, nn, e) in zip((w0, w1, w2), X_BLOCKS):
+            hi, lo = rh[0:m, n0 : n0 + nn], rl[0:m, n0 : n0 + nn]
+            b = jnp.dot(jnp.concatenate([hi, lo, hi, edge[e, 0:m]], axis=1), w[...], preferred_element_type=F32)
             for g in range(G):
                 for r0 in range(0, rows, 16):
                     for lb in range(nn // 128):
@@ -292,7 +319,7 @@
         for s in range(a, b):
             outs[s - 20].wait_recv()
         start_y(n)
-        start_x(n - 3)
+        start_x(n - 2)
 
     def meet(k, wait):
         far = 2**k
@@ -331,13 +358,15 @@
             @pl.when(d == n)
             def _(n=n):
                 wait_y(n)
+                if n == 1:
+                    wait_x(1)
 
         for n in (4, 5, 6):
 
             @pl.when(jnp.logical_and(d == n, has_outer))
             def _(n=n):
                 wait_y(n)
-                wait_x(n - 3)
+                wait_x(n - 2)
 
         chunk(0, d)
 
@@ -444,13 +473,14 @@
 
     for n in range(4):
         sent(y_copies(n))
-    sent(x_copies(0))
+    for n in range(2):
+        sent(x_copies(n))
 
     @pl.when(has_outer)
     def _():
         for n in (4, 5, 6):
             sent(y_copies(n))
-            sent(x_copies(n - 3))
+            sent(x_copies(n - 2))
 
 
 def shards(data_weight, blob_taps):
@@ -470,26 +500,27 @@
             pltpu.VMEM((G, 256, NX), BF16),
             pltpu.VMEM((G * ROWS, NX), BF16),
             pltpu.VMEM((G * ROWS, NX), BF16),
-            pltpu.VMEM((3 * 384, 256), BF16),
-            pltpu.VMEM((3 * 512, 256), BF16),
-            pltpu.VMEM((3 * 256, 128), BF16),
+            pltpu.VMEM((2, G * ROWS, 128), BF16),
+            pltpu.VMEM((3 * 256 + 128, 256), BF16),
+            pltpu.VMEM((3 * 256 + 128, 256), BF16),
+            pltpu.VMEM((3 * 128 + 128, 128), BF16),
             pltpu.VMEM((2 * ROWS, 256), BF16),
             pltpu.VMEM((3, 2, 8, 128), F32),
             pltpu.VMEM((2, XS, NX), F32),
             pltpu.VMEM((2, XS, NX), F32),
             pltpu.VMEM((len(REDUCE), 1, 128), F32),
-            pltpu.VMEM((len(REDUCE), 8, 1, 128), F32),
+            pltpu.VMEM((len(REDUCE), 32, 1, 128), F32),
             dma((NZ,)),
             dma((DEEP,)),
             dma((DEEP,)),
             dma((2, 7)),
             dma((2, 7)),
-            dma((2, 4)),
-            dma((2, 4)),
+            dma((2, 5)),
+            dma((2, 5)),
             dma((12,)),
             dma((12,)),
-            dma((len(REDUCE), 8)),
-            dma((len(REDUCE), 8)),
+            dma((len(REDUCE), 32)),
+            dma((len(REDUCE), 32)),
             pltpu.SemaphoreType.REGULAR((4,)),
             pltpu.SemaphoreType.REGULAR((2,)),
         ],

time: 74.2 us -> 65.3 us (0.88)
  Pallas kernels: 70.2 us -> 61.3 us
    pallas_call x1, Pallas kernels: 70.2 us -> 61.3 us  [shards(): pl.pallas_call(kernel, out_shape=(jax.ShapeDtypeStruct((NZ, NY, NX), F32)...]
where the time goes in v3:
time: 65.3 us; the launch traced here: 65.2 us
  Pallas kernels  61.3 us (94%)
  local copies, waits for them, and re-layouts  3.16 us (5%)
    pallas_call x1, Pallas kernels, shards(): pl.pallas_call(kernel, out_shape=(jax.ShapeDtypeStruct((NZ, NY, NX), F32)...  61.3 us
    unnamed x3, local copies, waits for them, and re-layouts  2.65 us

profile of v3, /device:TPU:1, one launch (start us, length us, event | category | flops | bytes accessed | tf_op | source)
XLA Modules:
  0.0 65.2 jit_solution(721665847091321049)
XLA Ops:
  0.6 0.0 copy-start
  0.6 0.7 %copy-done = f32[3,7]{1,0:T(4,128)S(1)} copy-done((f32[3,7]{1,0:T(4,128)S(1)}, f32[3,7]{1,0:T(4,128)}, u32[]{:S(2)}) %copy-start) | copy-done | bytes 108
  1.3 61.3 %shard_map.41 = (f32[20,80,640]{2,1,0:T(8,128)S(1)}, f32[1,128]{1,0:T(1,128)S(1)}) custom-call(f32[20,80,640]{2,1,0:T(8,128)} %bitcast.5, f32[3,7]{1,0:T(4,128)S(1)} %copy-done), custom_call_target="tpu_custom_call" | custom-call | tf_op jit(solution)/shard_map/pallas_call | solution.py:488
  62.7 0.5 slice_bitcast_fusion
  63.2 2.0 %copy.5 = f32[80,20,640]{2,0,1:T(8,128)} copy(f32[80,20,640]{2,0,1:T(8,128)S(1)} %bitcast.4) | data formatting | bytes 8192000
Async XLA Ops:
  0.6 0.7 %copy-start = (f32[3,7]{1,0:T(4,128)S(1)}, f32[3,7]{1,0:T(4,128)}, u32[]{:S(2)}) copy-start(f32[3,7]{1,0:T(4,128)} %taps.1) | copy-start | bytes 256

commit v4 on v3

--- a/solution.py
+++ b/solution.py
@@ -16,11 +16,10 @@
 G = 4
 ROWS = 96
 XR = 104
-Y_GROUPS = ((0, 7), (7, 11), (11, 15), (15, 20), (20, 23), (23, 27), (27, 29))
+Y_GROUPS = ((3, 7), (7, 11), (11, 15), (15, 20), (20, 23), (23, 27), (27, 29), (0, 3))
 X_GROUPS = ((0, 7, 0, 8), (7, 20, 8, 16), (20, 23, 24, 8), (23, 27, 32, 8), (27, 29, 40, 8))
 XS = 48
 TINY = 1e-30
-REDUCE = ((32, 1, "gz"), (8, 1, "gy"))
 X_BLOCKS = ((0, 256, 0), (256, 256, 1), (512, 128, 0))
 
 
@@ -46,16 +45,16 @@
     def plane(s):
         return core * s + (1 - core) * (NZ - 1 - s)
 
+    barrier = pltpu.get_barrier_semaphore()
+    for axis, me, size in (("gz", gz, nz), ("gy", gy, ny)):
+        for far in (1, size - 1):
+            pl.semaphore_signal(barrier, inc=1, device_id={axis: lax.rem(me + far, size)}, device_id_type=MESH)
+
     loads = [
         pltpu.make_async_copy(dw.at[plane(s)], p1.at[s + 3, 0:NY], load_sem.at[s]) for s in range(NZ)
     ]
     for copy in loads:
         copy.start()
-
-    barrier = pltpu.get_barrier_semaphore()
-    for axis, me, size in (("gz", gz, nz), ("gy", gy, ny)):
-        for far in (1, size - 1):
-            pl.semaphore_signal(barrier, inc=1, device_id={axis: lax.rem(me + far, size)}, device_id_type=MESH)
 
     p1[3:34, ROWS:XR, :] = jnp.zeros((31, XR - ROWS, NX), F32)
     p1[32:34, 0:ROWS, :] = jnp.zeros((2, ROWS, NX), F32)
@@ -166,6 +165,7 @@
     for s in range(7):
         loads[s].wait()
     start_x(0)
+    start_y(7)
     start_y(0)
 
     @pl.when(has_outer)
@@ -185,13 +185,15 @@
 
     tv = taps[...]
     tv = tv / jnp.sum(tv, axis=1, keepdims=True)
+    tv = [[tv[row : row + 1, k : k + 1] for k in range(7)] for row in range(3)]
     flip = core == 0
-    kz = [jnp.where(flip, tv[1:2, 6 - k : 7 - k], tv[1:2, k : k + 1]) for k in range(7)]
+    kz = [jnp.where(flip, tv[1][6 - k], tv[1][k]) for k in range(7)]
+    kr = [tap / kz[0] for tap in kz]
 
     def banded(diff):
         t = jnp.zeros(diff.shape, F32)
         for k in range(7):
-            t = jnp.where(diff == k - 3, tv[2:3, k : k + 1], t)
+            t = jnp.where(diff == k - 3, tv[2][k], t)
         return split(t)
 
     i = lax.broadcasted_iota(jnp.int32, (128, 128), 0)
@@ -221,7 +223,7 @@
     diff = yi - yo + 3
     t = jnp.zeros((ROWS, 128), F32)
     for k in range(7):
-        t = jnp.where(diff == k, tv[0:1, k : k + 1], t)
+        t = jnp.where(diff == k, tv[0][k] * kz[0], t)
     t_hi, t_lo = split(t)
     ay[0:ROWS, 0:128] = t_hi
     ay[0:ROWS, 128:256] = t_hi
@@ -235,27 +237,29 @@
         stat[t, 0] = jnp.zeros((8, 128), F32)
         stat[t, 1] = jnp.full((8, 128), 3e38, F32)
 
-    def chunk(t, d):
+    def chunk(t, d, count=G, gate=None):
         src = (p1, p2, p3)[t]
         base = d * G
         strips = 7 if t == 0 else 6
         for strip in range(strips):
             r0 = strip * 16
             height = 8 if strip == 6 else 16
+            if strip == 5 and gate is not None:
+                gate()
             for lb in range(5):
                 lanes = slice(lb * 128, (lb + 1) * 128)
-                p = [src[base + k, r0 : r0 + height, lanes] for k in range(G + 6)]
-                for g in range(G):
-                    acc = kz[0] * p[g]
+                p = [src[base + k, r0 : r0 + height, lanes] for k in range(count + 6)]
+                for g in range(count):
+                    acc = p[g]
                     for k in range(1, 7):
-                        acc = acc + kz[k] * p[g + k]
+                        acc = acc + kr[k] * p[g + k]
                     if height == 8:
                         acc = jnp.concatenate([acc, jnp.zeros((8, 128), F32)], axis=0)
                     hi, lo = split(acc)
                     q[g, r0 : r0 + 16, lanes] = hi
                     q[g, 128 + r0 : 144 + r0, lanes] = lo
         rows = 80 if t == 2 else ROWS
-        for g in range(G):
+        for g in range(count):
             if t == 2:
                 y = jnp.dot(ay[0:80, :], q[g], preferred_element_type=F32) + jnp.dot(
                     ay[ROWS : ROWS + 80, :], q[g], preferred_element_type=F32
@@ -279,13 +283,13 @@
                     jnp.where(lane < 11, pltpu.roll(rim - rim_hi, 8, 1), pltpu.roll(rim_hi, 16, 1)),
                 )
                 edge[e, at, :] = rim.astype(BF16)
-        m = G * rows
+        m = count * rows
         top = jnp.zeros((8, 128), F32)
         low = jnp.full((8, 128), 3e38, F32)
         for w, (n0, nn, e) in zip((w0, w1, w2), X_BLOCKS):
             hi, lo = rh[0:m, n0 : n0 + nn], rl[0:m, n0 : n0 + nn]
             b = jnp.dot(jnp.concatenate([hi, lo, hi, edge[e, 0:m]], axis=1), w[...], preferred_element_type=F32)
-            for g in range(G):
+            for g in range(count):
                 for r0 in range(0, rows, 16):
                     for lb in range(nn // 128):
                         v = b[g * rows + r0 : g * rows + r0 + 16, lb * 128 : (lb + 1) * 128]
@@ -300,7 +304,7 @@
                         else:
                             dst = (p2, p3)[t]
                             dst[base + 3 + g, r0 : r0 + 16, lanes] = p / jnp.maximum(v, TINY)
-        own = d * G < NZ
+        own = jnp.int32(d) * G < NZ
         stat[t, 0] = jnp.where(own, jnp.maximum(stat[t, 0], top), stat[t, 0])
         stat[t, 1] = jnp.where(own, jnp.minimum(stat[t, 1], low), stat[t, 1])
 
@@ -314,6 +318,15 @@
     inner_p3 = [
         remote(p3.at[3 + i], p3.at[2 - i], iss.at[9 + i], isr.at[9 + i], {"gz": inner}) for i in range(3)
     ]
+    def first_rims():
+        wait_x(0)
+        wait_y(7)
+        for copy in inner_rim:
+            copy.start()
+        wait_y(0)
+        for copy in inner_rim:
+            copy.wait_recv()
+
     def forward(n):
         a, b = Y_GROUPS[n]
         for s in range(a, b):
@@ -344,15 +357,6 @@
                 if k < 4:
                     meet(k, False)
 
-        @pl.when(d == 0)
-        def _():
-            wait_x(0)
-            wait_y(0)
-            for copy in inner_rim:
-                copy.start()
-            for copy in inner_own + inner_rim:
-                copy.wait_recv()
-
         for n in (1, 2, 3):
 
             @pl.when(d == n)
@@ -368,7 +372,19 @@
                 wait_y(n)
                 wait_x(n - 2)
 
-        chunk(0, d)
+        @pl.when(d == 0)
+        def _():
+            for copy in inner_own:
+                copy.wait_recv()
+            chunk(0, 0, gate=first_rims)
+
+        @pl.when(jnp.logical_and(d > 0, d < 6))
+        def _():
+            chunk(0, d)
+
+        @pl.when(d == 6)
+        def _():
+            chunk(0, d, 2)
 
         @pl.when(d == 0)
         def _():
@@ -386,9 +402,13 @@
             for copy in inner_p2:
                 copy.wait_recv()
 
-        @pl.when(d >= 1)
+        @pl.when(jnp.logical_and(d >= 1, d < 6))
         def _():
             chunk(1, d - 1)
+
+        @pl.when(d == 6)
+        def _():
+            chunk(1, d - 1, 3)
 
         @pl.when(d == 1)
         def _():
@@ -414,73 +434,69 @@
         worst = jnp.maximum(jnp.max(stat[t, 0]) - 1.0, 1.0 - jnp.min(stat[t, 1]))
         dev = jnp.where(lane == t, worst, dev)
 
+    def finish_sends():
+        for copy in inner_own + inner_rim + inner_p2 + inner_p3:
+            copy.wait_send()
+
+        @pl.when(has_outer)
+        def _():
+            for copy in outs:
+                copy.wait_send()
+
+        def sent(copies):
+            up, down = copies
+
+            @pl.when(has_up)
+            def _():
+                up.wait_send()
+
+            @pl.when(has_down)
+            def _():
+                down.wait_send()
+
+        for n in (0, 1, 2, 3, 7):
+            sent(y_copies(n))
+        for n in range(2):
+            sent(x_copies(n))
+
+        @pl.when(has_outer)
+        def _():
+            for n in (4, 5, 6):
+                sent(y_copies(n))
+                sent(x_copies(n - 2))
+
+    def group(stage):
+        if stage == 0:
+            far = [(dx, dy, dc) for dx in range(4) for dy in range(4) for dc in range(2)][1:]
+            far.sort(key=lambda s: -(min(s[0], 4 - s[0]) + min(s[1], 4 - s[1])))
+            x, y, c = gz // 8, lax.rem(gz // 2, 4), core
+            return "gz", gz, [lax.rem(x + dx, 4) * 8 + lax.rem(y + dy, 4) * 2 + lax.rem(c + dc, 2) for dx, dy, dc in far]
+        return "gy", gy, [lax.rem(gy + k, 8) for k in (4, 3, 5, 2, 6, 1, 7)]
+
     value = dev
-    for stage, (size, stride, axis) in enumerate(REDUCE):
-        me = gy if axis == "gy" else gz
-        member = lax.rem(me // stride, size)
-        seen[stage, member] = value
+    meanwhile = finish_sends
+    for stage in range(2):
+        axis, me, others = group(stage)
         mine[stage] = value
 
-        def copy(k):
-            other = lax.rem(member + k, size)
-            return remote(
-                mine.at[stage], seen.at[stage, member], rds.at[stage, k], rdr.at[stage, member],
-                {axis: me + (other - member) * stride},
-            )
-
-        def arrival(k):
-            other = lax.rem(member + k, size)
-            return remote(
-                mine.at[stage], seen.at[stage, other], rds.at[stage, k], rdr.at[stage, other],
-                {axis: me + (other - member) * stride},
-            )
-
-        for k in range(1, size):
-            copy(k).start()
-        for k in range(1, size):
-            arrival(k).wait_recv()
-        value = jnp.max(seen[stage, 0:size], axis=0)
-    for stage, (size, stride, axis) in enumerate(REDUCE):
-        me = gy if axis == "gy" else gz
-        member = lax.rem(me // stride, size)
-        for k in range(1, size):
-            other = lax.rem(member + k, size)
-            remote(
-                mine.at[stage], seen.at[stage, member], rds.at[stage, k], rdr.at[stage, member],
-                {axis: me + (other - member) * stride},
-            ).wait_send()
-    dev = value
-    dev_out[...] = dev
-
-    for copy in inner_own + inner_rim + inner_p2 + inner_p3:
-        copy.wait_send()
-
-    @pl.when(has_outer)
-    def _():
-        for copy in outs:
-            copy.wait_send()
-
-    def sent(copies):
-        up, down = copies
-
-        @pl.when(has_up)
-        def _():
-            up.wait_send()
-
-        @pl.when(has_down)
-        def _():
-            down.wait_send()
-
-    for n in range(4):
-        sent(y_copies(n))
-    for n in range(2):
-        sent(x_copies(n))
-
-    @pl.when(has_outer)
-    def _():
-        for n in (4, 5, 6):
-            sent(y_copies(n))
-            sent(x_copies(n - 2))
+        def copy(k, other, slot, stage=stage, axis=axis):
+            return remote(mine.at[stage], seen.at[stage, slot], rds.at[stage, k], rdr.at[stage, slot], {axis: other})
+
+        sends = [copy(k, other, me) for k, other in enumerate(others)]
+        for send in sends:
+            send.start()
+        seen[stage, me] = value
+        meanwhile()
+        for k, other in enumerate(others):
+            copy(k, other, other).wait_recv()
+        value = jnp.max(seen[stage, 0 : len(others) + 1], axis=0)
+
+        def meanwhile(sends=sends):
+            for send in sends:
+                send.wait_send()
+
+    dev_out[...] = value
+    meanwhile()
 
 
 def shards(data_weight, blob_taps):
@@ -508,19 +524,19 @@
             pltpu.VMEM((3, 2, 8, 128), F32),
             pltpu.VMEM((2, XS, NX), F32),
             pltpu.VMEM((2, XS, NX), F32),
-            pltpu.VMEM((len(REDUCE), 1, 128), F32),
-            pltpu.VMEM((len(REDUCE), 32, 1, 128), F32),
+            pltpu.VMEM((2, 1, 128), F32),
+            pltpu.VMEM((2, 32, 1, 128), F32),
             dma((NZ,)),
             dma((DEEP,)),
             dma((DEEP,)),
-            dma((2, 7)),
-            dma((2, 7)),
+            dma((2, 8)),
+            dma((2, 8)),
             dma((2, 5)),
             dma((2, 5)),
             dma((12,)),
             dma((12,)),
-            dma((len(REDUCE), 32)),
-            dma((len(REDUCE), 32)),
+            dma((2, 32)),
+            dma((2, 32)),
             pltpu.SemaphoreType.REGULAR((4,)),
             pltpu.SemaphoreType.REGULAR((2,)),
         ],

time: 65.3 us -> 63.3 us (0.969)
  Pallas kernels: 61.3 us -> 59.4 us
    pallas_call x1, Pallas kernels: 61.3 us -> 59.4 us  [shards(): pl.pallas_call(kernel, out_shape=(jax.ShapeDtypeStruct((NZ, NY, NX), F32)...]
where the time goes in v4:
time: 63.3 us; the launch traced here: 63.2 us
  Pallas kernels  59.4 us (94%)
  local copies, waits for them, and re-layouts  3.16 us (5%)
  between operations  0.65 us (1%)
    pallas_call x1, Pallas kernels, shards(): pl.pallas_call(kernel, out_shape=(jax.ShapeDtypeStruct((NZ, NY, NX), F32)...  59.4 us
    unnamed x3, local copies, waits for them, and re-layouts  2.65 us

profile of v4, /device:TPU:1, one launch (start us, length us, event | category | flops | bytes accessed | tf_op | source)
XLA Modules:
  0.0 63.2 jit_solution(14470584099932668873)
XLA Ops:
  0.6 0.0 copy-start
  0.6 0.7 %copy-done = f32[3,7]{1,0:T(4,128)S(1)} copy-done((f32[3,7]{1,0:T(4,128)S(1)}, f32[3,7]{1,0:T(4,128)}, u32[]{:S(2)}) %copy-start) | copy-done | bytes 108
  1.3 59.4 %shard_map.41 = (f32[20,80,640]{2,1,0:T(8,128)S(1)}, f32[1,128]{1,0:T(1,128)S(1)}) custom-call(f32[20,80,640]{2,1,0:T(8,128)} %bitcast.5, f32[3,7]{1,0:T(4,128)S(1)} %copy-done), custom_call_target="tpu_custom_call" | custom-call | tf_op jit(solution)/shard_map/pallas_call | solution.py:504
  60.7 0.5 slice_bitcast_fusion
  61.2 2.0 %copy.5 = f32[80,20,640]{2,0,1:T(8,128)} copy(f32[80,20,640]{2,0,1:T(8,128)S(1)} %bitcast.4) | data formatting | bytes 8192000
Async XLA Ops:
  0.6 0.7 %copy-start = (f32[3,7]{1,0:T(4,128)S(1)}, f32[3,7]{1,0:T(4,128)}, u32[]{:S(2)}) copy-start(f32[3,7]{1,0:T(4,128)} %taps.1) | copy-start | bytes 256

commit v5 on v4

--- a/solution.py
+++ b/solution.py
@@ -20,6 +20,7 @@
 X_GROUPS = ((0, 7, 0, 8), (7, 20, 8, 16), (20, 23, 24, 8), (23, 27, 32, 8), (27, 29, 40, 8))
 XS = 48
 TINY = 1e-30
+EARLY = 4
 X_BLOCKS = ((0, 256, 0), (256, 256, 1), (512, 128, 0))
 
 
@@ -230,22 +231,21 @@
     ay[ROWS : 2 * ROWS, 0:128] = t_lo
     ay[ROWS : 2 * ROWS, 128:256] = jnp.zeros((ROWS, 128), BF16)
 
-    for g in range(G):
+    def clear_q(g, carry):
         q[g, 96:128, :] = jnp.zeros((32, NX), BF16)
         q[g, 224:256, :] = jnp.zeros((32, NX), BF16)
+        return carry
+
+    lax.fori_loop(0, EARLY * G, clear_q, 0)
     for t in range(3):
         stat[t, 0] = jnp.zeros((8, 128), F32)
         stat[t, 1] = jnp.full((8, 128), 3e38, F32)
 
-    def chunk(t, d, count=G, gate=None):
+    def smear_z(t, base, strips, count, qb):
         src = (p1, p2, p3)[t]
-        base = d * G
-        strips = 7 if t == 0 else 6
-        for strip in range(strips):
+        for strip in strips:
             r0 = strip * 16
             height = 8 if strip == 6 else 16
-            if strip == 5 and gate is not None:
-                gate()
             for lb in range(5):
                 lanes = slice(lb * 128, (lb + 1) * 128)
                 p = [src[base + k, r0 : r0 + height, lanes] for k in range(count + 6)]
@@ -256,16 +256,22 @@
                     if height == 8:
                         acc = jnp.concatenate([acc, jnp.zeros((8, 128), F32)], axis=0)
                     hi, lo = split(acc)
-                    q[g, r0 : r0 + 16, lanes] = hi
-                    q[g, 128 + r0 : 144 + r0, lanes] = lo
+                    q[qb + g, r0 : r0 + 16, lanes] = hi
+                    q[qb + g, 128 + r0 : 144 + r0, lanes] = lo
+
+    def chunk(t, d, count=G, early=False):
+        src = (p1, p2, p3)[t]
+        base = d * G
+        qb = base if early else 0
+        smear_z(t, base, range(5 if early else 0, 7 if t == 0 else 6), count, qb)
         rows = 80 if t == 2 else ROWS
         for g in range(count):
             if t == 2:
-                y = jnp.dot(ay[0:80, :], q[g], preferred_element_type=F32) + jnp.dot(
-                    ay[ROWS : ROWS + 80, :], q[g], preferred_element_type=F32
+                y = jnp.dot(ay[0:80, :], q[qb + g], preferred_element_type=F32) + jnp.dot(
+                    ay[ROWS : ROWS + 80, :], q[qb + g], preferred_element_type=F32
                 )
             else:
-                y = jnp.dot(ay[...], q[g], preferred_element_type=F32)
+                y = jnp.dot(ay[...], q[qb + g], preferred_element_type=F32)
                 y = y[0:ROWS] + y[ROWS : 2 * ROWS]
             hi, lo = split(y)
             at = slice(g * rows, (g + 1) * rows)
@@ -357,6 +363,10 @@
                 if k < 4:
                     meet(k, False)
 
+        @pl.when(d == 0)
+        def _():
+            first_rims()
+
         for n in (1, 2, 3):
 
             @pl.when(d == n)
@@ -372,13 +382,11 @@
                 wait_y(n)
                 wait_x(n - 2)
 
-        @pl.when(d == 0)
-        def _():
-            for copy in inner_own:
-                copy.wait_recv()
-            chunk(0, 0, gate=first_rims)
-
-        @pl.when(jnp.logical_and(d > 0, d < 6))
+        @pl.when(d < EARLY)
+        def _():
+            chunk(0, d, early=True)
+
+        @pl.when(jnp.logical_and(d >= EARLY, d < 6))
         def _():
             chunk(0, d)
 
@@ -426,6 +434,14 @@
 
         return carry
 
+    for copy in inner_own:
+        copy.wait_recv()
+
+    def own_rows(d, carry):
+        smear_z(0, d * G, range(5), G, d * G)
+        return carry
+
+    lax.fori_loop(0, EARLY, own_rows, 0)
     lax.fori_loop(0, 7, wave, 0)
 
     lane = lax.broadcasted_iota(jnp.int32, (1, 128), 1)
@@ -513,7 +529,7 @@
             pltpu.VMEM((34, XR, NX), F32),
             pltpu.VMEM((31, ROWS, NX), F32),
             pltpu.VMEM((27, ROWS, NX), F32),
-            pltpu.VMEM((G, 256, NX), BF16),
+            pltpu.VMEM((EARLY * G, 256, NX), BF16),
             pltpu.VMEM((G * ROWS, NX), BF16),
             pltpu.VMEM((G * ROWS, NX), BF16),
             pltpu.VMEM((2, G * ROWS, 128), BF16),

time: 63.3 us -> 61.7 us (0.975)
  Pallas kernels: 59.4 us -> 57.8 us
    pallas_call x1, Pallas kernels: 59.4 us -> 57.8 us  [shards(): pl.pallas_call(kernel, out_shape=(jax.ShapeDtypeStruct((NZ, NY, NX), F32)...]
where the time goes in v5:
time: 61.7 us; the launch traced here: 61.6 us
  Pallas kernels  57.8 us (94%)
  local copies, waits for them, and re-layouts  3.16 us (5%)
  between operations  0.65 us (1%)
    pallas_call x1, Pallas kernels, shards(): pl.pallas_call(kernel, out_shape=(jax.ShapeDtypeStruct((NZ, NY, NX), F32)...  57.8 us
    unnamed x3, local copies, waits for them, and re-layouts  2.65 us

profile of v5, /device:TPU:1, one launch (start us, length us, event | category | flops | bytes accessed | tf_op | source)
XLA Modules:
  0.0 61.6 jit_solution(15017653083863602490)
XLA Ops:
  0.6 0.0 copy-start
  0.6 0.7 %copy-done = f32[3,7]{1,0:T(4,128)S(1)} copy-done((f32[3,7]{1,0:T(4,128)S(1)}, f32[3,7]{1,0:T(4,128)}, u32[]{:S(2)}) %copy-start) | copy-done | bytes 108
  1.3 57.8 %shard_map.41 = (f32[20,80,640]{2,1,0:T(8,128)S(1)}, f32[1,128]{1,0:T(1,128)S(1)}) custom-call(f32[20,80,640]{2,1,0:T(8,128)} %bitcast.5, f32[3,7]{1,0:T(4,128)S(1)} %copy-done), custom_call_target="tpu_custom_call" | custom-call | tf_op jit(solution)/shard_map/pallas_call | solution.py:520
  59.1 0.5 slice_bitcast_fusion
  59.6 2.0 %copy.5 = f32[80,20,640]{2,0,1:T(8,128)} copy(f32[80,20,640]{2,0,1:T(8,128)S(1)} %bitcast.4) | data formatting | bytes 8192000
Async XLA Ops:
  0.6 0.7 %copy-start = (f32[3,7]{1,0:T(4,128)S(1)}, f32[3,7]{1,0:T(4,128)}, u32[]{:S(2)}) copy-start(f32[3,7]{1,0:T(4,128)} %taps.1) | copy-start | bytes 256
